TPU v7x, 64 devices: a 2x2x8 block of a 4x4x8 slice. The times are simulated.
64 devices in a mesh: dp: 8 (over x, y, core), tp: 8 (over z).
Axes of the slice: x: 2, y: 2, z: 8, core: 2. Of those that a mesh axis runs over, the one named last changes fastest.
The devices are a block of a 4x4x8 slice.
Arguments:
- x: bfloat16 [512, 2048], P('dp'), parts along dimension 0
- k_cache: bfloat16 [512, 1024, 16, 128], P('dp', None, 'tp'), parts along dimension 0
- v_cache: bfloat16 [512, 1024, 16, 128], P('dp', None, 'tp'), parts along dimension 0
- gain_a: bfloat16 [2048], replicated
- wq: bfloat16 [2048, 2048], P(None, 'tp')
- wo: bfloat16 [2048, 2048], P('tp')
- gain_m: bfloat16 [2048], replicated
- w_gate: bfloat16 [2048, 8192], P(None, 'tp')
- w_up: bfloat16 [2048, 8192], P(None, 'tp')
- w_down: bfloat16 [8192, 2048], P('tp')
Outputs:
- output: bfloat16 [512, 2048], P('dp'), parts along dimension 0
There are 8 independent parts. A program takes and returns all parts, laid end to end along the dimension named above; an argument that names none is the same for every part.
All inputs are finite; a program needn't handle non-finite values.
Results may differ from a plain program's by a relative error of at most 0.017.
Values are sent between devices in bfloat16 or wider.
A program may use at most 768 MiB of HBM per device.

v0:
```python
import jax
import jax.numpy as jnp
from jax import lax
from jax.sharding import PartitionSpec as P

HEAD = 128
THETA = 10000


def normed(x, gain):
    wide = x.astype(jnp.float32)
    scale = lax.rsqrt(jnp.mean(wide * wide, -1, keepdims=True) + 1e-6)
    return (wide * scale * gain.astype(jnp.float32)).astype(jnp.bfloat16)


def turned(t, place, theta):
    half = t.shape[-1] // 2
    angle = place.astype(jnp.float32)[:, None] * theta ** (-jnp.arange(half, dtype=jnp.float32) / half)
    cos, sin = jnp.cos(angle)[:, None], jnp.sin(angle)[:, None]
    a, b = t[..., :half].astype(jnp.float32), t[..., half:].astype(jnp.float32)
    return jnp.concatenate([a * cos - b * sin, b * cos + a * sin], -1).astype(jnp.bfloat16)


def matmul(a, w):
    return jnp.dot(a, w, preferred_element_type=jnp.float32).astype(jnp.bfloat16)


def einsum(form, a, b):
    return jnp.einsum(form, a.astype(jnp.float32), b.astype(jnp.float32))


def seen_by(a, wq, k_cache, v_cache, head, theta):
    batch, cache, kv_heads = k_cache.shape[:3]
    place = jnp.full((batch,), cache - 1)
    q = turned(matmul(a, wq).reshape(batch, -1, head), place, theta).reshape(batch, kv_heads, -1, head)
    scores = einsum("bgsd,bugd->bgsu", q, k_cache) * head**-0.5
    weights = jax.nn.softmax(scores, -1).astype(jnp.bfloat16)
    return einsum("bgsu,bugd->bgsd", weights, v_cache).astype(jnp.bfloat16).reshape(batch, -1)


def hidden_of(b, w_gate, w_up):
    gate = jnp.dot(b, w_gate, preferred_element_type=jnp.float32)
    up = jnp.dot(b, w_up, preferred_element_type=jnp.float32)
    return (jax.nn.silu(gate) * up).astype(jnp.bfloat16)


def solution(mesh):
    def added(t, term):
        return (t.astype(jnp.float32) + lax.psum(term.astype(jnp.bfloat16), "tp").astype(jnp.float32)).astype(jnp.bfloat16)

    def step(x, k_cache, v_cache, gain_a, wq, wo, gain_m, w_gate, w_up, w_down):
        seen = seen_by(normed(x, gain_a), wq, k_cache, v_cache, HEAD, THETA)
        h = added(x, jnp.dot(seen, wo, preferred_element_type=jnp.float32))
        return added(h, jnp.dot(hidden_of(normed(h, gain_m), w_gate, w_up), w_down, preferred_element_type=jnp.float32))

    states, cache, columns, rows_of = P("dp", None), P("dp", None, "tp", None), P(None, "tp"), P("tp", None)
    return jax.shard_map(
        step,
        mesh=mesh,
        in_specs=(states, cache, cache, P(None), columns, rows_of, P(None), columns, columns, rows_of),
        out_specs=states,
        check_vma=False,
    )
```

profile of v0, /device:TPU:22, one launch (start us, length us, event | category | flops | bytes accessed | tf_op | source)
XLA Modules:
  0.0 197.6 jit_solution(5435512017222996625)
XLA Ops:
  6.5 0.0 copy-start
  6.6 0.0 all-reduce.3.cloned.1.call-start
  6.6 1.2 fusion.12
  7.8 0.7 convert_element_type.66
  8.5 1.7 convolution_convert_fusion.2
  10.2 0.1 fusion.51
  10.3 0.1 maximum_bitcast_fusion
  10.4 16.6 %fusion.4 = f32[64,2,1,1024]{3,2,1,0:T(1,128)S(1)} fusion(bf16[64,1024,2,128]{3,2,1,0:T(2,128)(2,1)} %param.11, bf16[64,2,128,1]{2,0,1,3:T(8,128)(2,1)S(1)} %maximum_bitcast_fusion), kind=kOutput, calls=%fused_computation.4 | convolution fusion | flops 33554432 | bytes 34111488 | tf_op jit(solution)/shard_map/bgsd,bugd->bgsu/dot_general | solution.py:29
  27.0 0.5 fusion.10
  27.5 0.0 copy-start.2
  27.5 0.0 copy-start.1
  27.5 15.1 %fusion.2 = f32[64,2,1,128]{3,2,1,0:T(1,128)S(1)} fusion(bf16[64,1024,2,128]{3,2,1,0:T(2,128)(2,1)} %param.12, bf16[64,2,1024,1]{2,0,1,3:T(8,128)(2,1)S(1)} %fusion.10), kind=kOutput, calls=%fused_computation.2 | convolution fusion | flops 33554432 | bytes 33882112 | tf_op jit(solution)/shard_map/bgsu,bugd->bgsd/dot_general | solution.py:29
  42.7 0.0 copy-done
  42.7 1.0 convolution_convert_fusion
  43.7 0.1 all-reduce.3.cloned.1.call-update
  43.8 0.1 all-reduce.5.cloned.1.call-start
  43.8 0.0 copy-done.2
  43.9 70.2 %all-reduce.3.cloned.1.call-done = bf16[64,2048]{1,0:T(8,128)(2,1)} async-done(((bf16[64,2048]{1,0:T(8,128)(2,1)}), bf16[64,2048]{1,0:T(8,128)(2,1)}) %all-reduce.3.cloned.1.call-update) | async-done | bytes 262160 | tf_op jit(solution)/shard_map/psum | solution.py:49
  114.0 0.0 copy-done.1
  114.0 1.1 fusion.16
  115.2 3.1 %fusion.34 = f32[64,1024]{1,0:T(8,128)S(1)} fusion(bf16[2048,1024]{1,0:T(8,128)(2,1)} %param.17, bf16[64,2048]{1,0:T(8,128)(2,1)S(1)} %get-tuple-element.6, f32[2048]{0:T(1024)S(1)} %convert_element_type.77, f32[64]{0:T(128)S(1)} %add_rsqrt_fusion), kind=kOutput, calls=%fused_computation.46 | convolution fusion | flops 268959744 | bytes 4727040 | tf_op jit(solution)/shard_map/dot_general | solution.py:42
  118.3 5.8 %convolution_convert_fusion.1 = bf16[64,2048]{1,0:T(8,128)(2,1)} fusion(bf16[1024,2048]{1,0:T(8,128)(2,1)} %param.19, bf16[2048,1024]{1,0:T(8,128)(2,1)} %param.18, f32[64,1024]{1,0:T(8,128)S(1)} %fusion.34, bf16[64,2048]{1,0:T(8,128)(2,1)S(1)} %get-tuple-element.6, f32[2048]{0:T(1024)S(1)} %convert_element_type.77, f32[64]{0:T(128)S(1)} %add_rsqrt_fusion), kind=kOutput, calls=%fused_computation.7 | convolution fusion | flops 537919488 | bytes 9183488 | tf_op jit(solution)/shard_map/dot_general | solution.py:54
  124.1 0.1 all-reduce.5.cloned.1.call-update
  124.1 64.8 %all-reduce.5.cloned.1.call-done = bf16[64,2048]{1,0:T(8,128)(2,1)} async-done(((bf16[64,2048]{1,0:T(8,128)(2,1)}), bf16[64,2048]{1,0:T(8,128)(2,1)}) %all-reduce.5.cloned.1.call-update) | async-done | bytes 262160 | tf_op jit(solution)/shard_map/psum | solution.py:49
  189.0 1.7 fusion.19
  (7 shorter events, 0.1 us)
Async XLA Ops:
  6.5 36.1 %copy-start = (bf16[256,2048]{1,0:T(8,128)(2,1)S(1)}, bf16[256,2048]{1,0:T(8,128)(2,1)}, u32[]{:S(2)}) copy-start(bf16[256,2048]{1,0:T(8,128)(2,1)} %param.15) | copy-start | bytes 3145732
  6.6 107.5 %all-reduce.3.cloned.1.call-start = ((), (), s32[]{:S(2)}) async-start(), calls=%async_computation | async-start | bytes 524288 | tf_op jit(solution)/shard_map/psum | solution.py:49
  27.5 16.4 %copy-start.2 = (bf16[2048]{0:T(1024)(128)(2,1)S(1)}, bf16[2048]{0:T(1024)(128)(2,1)}, u32[]{:S(2)}) copy-start(bf16[2048]{0:T(1024)(128)(2,1)} %param.16) | copy-start | bytes 12292
  27.5 86.5 %copy-start.1 = (bf16[64,2048]{1,0:T(8,128)(2,1)S(1)}, bf16[64,2048]{1,0:T(8,128)(2,1)}, u32[]{:S(2)}) copy-start(bf16[64,2048]{1,0:T(8,128)(2,1)} %param.10) | copy-start | bytes 786436
  43.8 145.2 %all-reduce.5.cloned.1.call-start = ((), (), s32[]{:S(2)}) async-start(), calls=%async_computation.1 | async-start | bytes 524288 | tf_op jit(solution)/shard_map/psum | solution.py:49
Sparse Core Ops, SparseCore 0:
  43.9 70.0 all-reduce.2
  124.3 64.6 all-reduce.4
where the time goes:
time: 198 us
  waiting for transfers between devices  135 us (68%)
  matrix products  43.2 us (22%)
  between operations  13.5 us (7%)
  other arithmetic  5.44 us (3%)
    psum x2, waiting for transfers between devices, added(): lax.psum(term.astype(jnp.bfloat16), 'tp').astype(jnp.float32)  135 us
    dot_general x2, matrix products, einsum(): return jnp.einsum(form, a.astype(jnp.float32), b.astype(jnp.float32))  31.7 us
    dot_general x1, matrix products, step(): jnp.dot(hidden_of(normed(h, gain_m), w_gate, w_up), w_down, preferred_ele...  5.81 us
  transfers between devices with their start and end apart: 2, of which 2 were waited for; matrix products, arithmetic and copies ran while one was open for 0% of the time, Pallas kernels for 0%

commit v1 on v0

v1 whole, which is shorter than its diff:
```python
import functools

import jax
import jax.numpy as jnp
import numpy as np
from jax import lax
from jax.experimental import pallas as pl
from jax.experimental.pallas import tpu as pltpu
from jax.sharding import PartitionSpec as P

HEAD = 128
THETA = 10000
F32, BF16 = jnp.float32, jnp.bfloat16

CH = 8
SLOTS = 4
LAG = 3


def dot(a, b):
    return lax.dot_general(a, b, (((1,), (0,)), ((), ())), preferred_element_type=F32)


def dot_t(a, b):
    return lax.dot_general(a, b, (((1,), (1,)), ((), ())), preferred_element_type=F32)


def kernel(n, x_hbm, k_hbm, v_hbm, ga_hbm, wq_hbm, wo_hbm, gm_hbm, wg_hbm, wu_hbm, wd_hbm, cs_hbm, y_ref,
           xb, xf, ga, gm, cs, wq, wo, wg, wu, wd, kbuf, vbuf, qf, pf, sbuf, rbuf, hbuf, bbuf, p2, s2, r2, ybuf,
           sem_in, sem_k, sem_v, rs_s, rs_r, ag_s, ag_r, rs2_s, rs2_r, ag2_s, ag2_r):
    me = lax.axis_index("tp")
    rows, d = xb.shape
    chunks = rows // CH
    blk = d // n
    span = kbuf.shape[2] // 2

    def peer(j):
        return lax.rem(me + j, n)

    def load(i, src, dst):
        return pltpu.make_async_copy(src, dst, sem_in.at[i])

    first = [load(0, x_hbm, xb), load(1, ga_hbm, ga), load(2, cs_hbm, cs), load(3, wq_hbm, wq)]
    second = [load(4, wo_hbm, wo), load(5, gm_hbm, gm)]
    third = [load(6, wg_hbm, wg), load(7, wu_hbm, wu), load(8, wd_hbm, wd)]

    def fetch_k(c, slot):
        return pltpu.make_async_copy(k_hbm.at[pl.ds(c * CH, CH)], kbuf.at[slot], sem_k.at[slot])

    def fetch_v(c, slot):
        return pltpu.make_async_copy(v_hbm.at[pl.ds(c * CH, CH)], vbuf.at[slot], sem_v.at[slot])

    for cp in first:
        cp.start()
    fetch_k(0, 0).start()
    fetch_v(0, 0).start()
    for cp in second:
        cp.start()
    for c in range(1, SLOTS):
        fetch_k(c, c).start()
        fetch_v(c, c).start()

    barrier = pltpu.get_barrier_semaphore()
    for j in range(1, n):
        pl.semaphore_signal(barrier, inc=1, device_id={"tp": peer(j)})

    for cp in first[:3]:
        cp.wait()
    xv = xb[...].astype(F32)
    xf[...] = xv
    scale = lax.rsqrt(jnp.sum(xv * xv, -1, keepdims=True) * (1.0 / d) + 1e-6)
    gav = ga[...].astype(F32)
    for i in range(d // 128):
        at = slice(128 * i, 128 * i + 128)
        bbuf[:, at] = (xf[:, at] * scale * gav[i:i + 1]).astype(BF16)
    first[3].wait()
    q = dot(bbuf[...], wq[...]).astype(BF16).astype(F32)
    for g in range(2):
        t = q[:, HEAD * g:HEAD * (g + 1)]
        turned = t * cs[0:1] + pltpu.roll(t, HEAD // 2, 1) * cs[1:2]
        qf[:, HEAD * g:HEAD * (g + 1)] = turned.astype(BF16).astype(F32)

    for cp in second:
        cp.wait()
    pl.semaphore_wait(barrier, n - 1)

    def rs_copy(c, j):
        return pltpu.make_async_remote_copy(
            src_ref=sbuf.at[c, peer(j)], dst_ref=rbuf.at[c, j - 1], send_sem=rs_s.at[c], recv_sem=rs_r.at[c],
            device_id={"tp": peer(j)})

    def ag_copy(c, j):
        return pltpu.make_async_remote_copy(
            src_ref=hbuf.at[c, me], dst_ref=hbuf.at[c, me], send_sem=ag_s.at[c], recv_sem=ag_r.at[c],
            device_id={"tp": peer(j)})

    def all_of(ref, sem):
        pltpu.make_async_copy(ref, ref, sem).wait()

    def finish(c):
        all_of(rbuf.at[c], rs_r.at[c])
        total = pf[c, me]
        for j in range(n - 1):
            total = total + rbuf[c, j].astype(F32)
        total = total + xf[pl.ds(pl.multiple_of(c * CH, CH), CH), pl.ds(pl.multiple_of(me * blk, blk), blk)]
        hbuf[c, me] = total.astype(BF16)
        for j in range(1, n):
            ag_copy(c, j).start()

    row = lax.broadcasted_iota(jnp.int32, (4 * CH, 256), 0)
    row_w = lax.broadcasted_iota(jnp.int32, (4 * CH, span), 0)
    col_w = lax.broadcasted_iota(jnp.int32, (4 * CH, span), 1)
    seen_by_row = (col_w % 2) == ((row_w // CH) % 2)

    def attend(c, _):
        slot = lax.rem(c, SLOTS)
        fetch_k(c, slot).wait()
        qc = qf[pl.ds(pl.multiple_of(c * CH, CH), CH), :]
        q0, q1 = qc[:, :HEAD], qc[:, HEAD:]
        zero = jnp.zeros_like(q0)
        base = jnp.concatenate([jnp.concatenate([q0, q1, zero, zero], 0), jnp.concatenate([zero, zero, q0, q1], 0)], 1)
        s = None
        for i in range(CH):
            lhs = jnp.where(row % CH == i, base, 0.0).astype(BF16)
            keys = jnp.concatenate([kbuf[slot, i, :span], kbuf[slot, i, span:]], 1)
            t = dot_t(lhs, keys)
            s = t if s is None else s + t
        s = jnp.where(seen_by_row, s * HEAD**-0.5, -jnp.inf)
        m = jnp.max(s, -1, keepdims=True)
        m = jnp.maximum(m[:2 * CH], m[2 * CH:])
        m = jnp.concatenate([m, m], 0)
        e = jnp.exp(s - m)
        z = jnp.sum(e, -1, keepdims=True)
        z = z[:2 * CH] + z[2 * CH:]
        z = 1.0 / jnp.concatenate([z, z], 0)
        w = e * z
        fetch_v(c, slot).wait()
        o = None
        for i in range(CH):
            lhs = jnp.where(row_w % CH == i, w, 0.0).astype(BF16)
            values = jnp.concatenate([vbuf[slot, i, :span], vbuf[slot, i, span:]], 1)
            t = dot(lhs, values)
            o = t if o is None else o + t
        o = o[:2 * CH, :HEAD] + o[2 * CH:, HEAD:]
        seen = jnp.concatenate([o[:CH], o[CH:]], 1).astype(BF16)

        @pl.when(c + SLOTS < chunks)
        def _():
            fetch_k(c + SLOTS, slot).start()
            fetch_v(c + SLOTS, slot).start()

        @pl.when(c + SLOTS == chunks)
        def _():
            for cp in third:
                cp.start()

        term = dot(seen, wo[...])
        for j in range(n):
            part = term[:, blk * j:blk * (j + 1)]
            pf[c, j] = part
            sbuf[c, j] = part.astype(BF16)
        for j in range(1, n):
            rs_copy(c, j).start()

        @pl.when(c >= LAG)
        def _():
            finish(c - LAG)

        return 0

    lax.fori_loop(0, chunks, attend, 0)
    for c in range(chunks - LAG, chunks):
        finish(c)
    for cp in third:
        cp.wait()

    for c in range(chunks):
        all_of(rbuf.at[c], ag_r.at[c])
    gmv = gm[...].astype(F32)

    def h_block(j):
        return hbuf[:, j].astype(F32).reshape(rows, blk)

    total = None
    for j in range(n):
        hj = h_block(j)
        t = jnp.sum(hj * hj, -1, keepdims=True)
        total = t if total is None else total + t
    scale = lax.rsqrt(total * (1.0 / d) + 1e-6)
    for j in range(n):
        hj = h_block(j)
        for i in range(blk // 128):
            g = j * (blk // 128) + i
            bbuf[:, 128 * g:128 * g + 128] = (hj[:, 128 * i:128 * i + 128] * scale * gmv[g:g + 1]).astype(BF16)
    hidden = []
    for f in range(wg.shape[1] // 256):
        at = slice(256 * f, 256 * f + 256)
        gate = dot(bbuf[...], wg[:, at])
        up = dot(bbuf[...], wu[:, at])
        hidden.append((jax.nn.silu(gate) * up).astype(BF16))
    hidden = jnp.concatenate(hidden, 1)

    def rs2_copy(j):
        return pltpu.make_async_remote_copy(
            src_ref=s2.at[peer(j)], dst_ref=r2.at[j - 1], send_sem=rs2_s, recv_sem=rs2_r, device_id={"tp": peer(j)})

    def ag2_copy(j):
        return pltpu.make_async_remote_copy(
            src_ref=ybuf.at[me], dst_ref=ybuf.at[me], send_sem=ag2_s, recv_sem=ag2_r, device_id={"tp": peer(j)})

    for j in range(n):
        part = dot(hidden, wd[:, blk * j:blk * (j + 1)])
        p2[j] = part
        s2[j] = part.astype(BF16)
    for j in range(1, n):
        rs2_copy(j).start()
    all_of(r2, rs2_r)
    total = p2[me]
    for j in range(n - 1):
        total = total + r2[j].astype(F32)
    total = total + hbuf[:, me].astype(F32).reshape(rows, blk)
    ybuf[me] = total.astype(BF16)
    for j in range(1, n):
        ag2_copy(j).start()
    for c in range(chunks):
        all_of(rbuf.at[c], rs_s.at[c])
        all_of(rbuf.at[c], ag_s.at[c])
    all_of(r2, rs2_s)
    all_of(r2, ag2_r)
    all_of(r2, ag2_s)
    for j in range(n):
        y_ref[:, blk * j:blk * (j + 1)] = ybuf[j]


def solution(mesh):
    n = mesh.shape["tp"]

    def step(x, k_cache, v_cache, gain_a, wq, wo, gain_m, w_gate, w_up, w_down):
        rows, d = x.shape
        batch, cache, heads, head = k_cache.shape
        ff = w_gate.shape[1]
        chunks, blk = rows // CH, d // n
        half = head // 2
        angle = (cache - 1) * float(THETA) ** (-np.arange(half) / half)
        cos, sin = np.cos(angle), np.sin(angle)
        cs = np.zeros((8, head), np.float32)
        cs[0], cs[1] = np.concatenate([cos, cos]), np.concatenate([-sin, sin])
        keys = k_cache.reshape(batch, cache * heads, head)
        values = v_cache.reshape(batch, cache * heads, head)
        dma = pltpu.SemaphoreType.DMA
        return pl.pallas_call(
            functools.partial(kernel, n),
            out_shape=jax.ShapeDtypeStruct((rows, d), BF16),
            in_specs=[pl.BlockSpec(memory_space=pl.ANY)] * 11,
            out_specs=pl.BlockSpec(memory_space=pltpu.VMEM),
            scratch_shapes=[
                pltpu.VMEM((rows, d), BF16),
                pltpu.VMEM((rows, d), F32),
                pltpu.VMEM((d // 128, 128), BF16),
                pltpu.VMEM((d // 128, 128), BF16),
                pltpu.VMEM((8, head), F32),
                pltpu.VMEM(wq.shape, BF16),
                pltpu.VMEM(wo.shape, BF16),
                pltpu.VMEM(w_gate.shape, BF16),
                pltpu.VMEM(w_up.shape, BF16),
                pltpu.VMEM(w_down.shape, BF16),
                pltpu.VMEM((SLOTS, CH, cache * heads, head), BF16),
                pltpu.VMEM((SLOTS, CH, cache * heads, head), BF16),
                pltpu.VMEM((rows, heads * head), F32),
                pltpu.VMEM((chunks, n, CH, blk), F32),
                pltpu.VMEM((chunks, n, CH, blk), BF16),
                pltpu.VMEM((chunks, n - 1, CH, blk), BF16),
                pltpu.VMEM((chunks, n, CH, blk), BF16),
                pltpu.VMEM((rows, d), BF16),
                pltpu.VMEM((n, rows, blk), F32),
                pltpu.VMEM((n, rows, blk), BF16),
                pltpu.VMEM((n - 1, rows, blk), BF16),
                pltpu.VMEM((n, rows, blk), BF16),
                dma((9,)), dma((SLOTS,)), dma((SLOTS,)),
                dma((chunks,)), dma((chunks,)), dma((chunks,)), dma((chunks,)),
                dma(()), dma(()), dma(()), dma(()),
            ],
            compiler_params=pltpu.CompilerParams(
                collective_id=0, has_side_effects=True, vmem_limit_bytes=64 * 1024 * 1024 - 65536),
            name="decoder_layer",
        )(x, keys, values, gain_a.reshape(d // 128, 128), wq, wo, gain_m.reshape(d // 128, 128), w_gate, w_up, w_down, jnp.asarray(cs))

    states, cache, columns, rows_of = P("dp", None), P("dp", None, "tp", None), P(None, "tp"), P("tp", None)
    return jax.shard_map(
        step,
        mesh=mesh,
        in_specs=(states, cache, cache, P(None), columns, rows_of, P(None), columns, columns, rows_of),
        out_specs=states,
        check_vma=False,
    )
```

time: 198 us -> 73.9 us (0.37)
  waiting for transfers between devices: 135 us -> 0 us
  Pallas kernels: 0 us -> 71.4 us
  matrix products: 43.2 us -> 0 us
  between operations: 13.5 us -> 0.01 us
  other arithmetic: 5.44 us -> 0 us
    psum x2 -> x0, waiting for transfers between devices: 135 us -> none  [added(): lax.psum(term.astype(jnp.bfloat16), 'tp').astype(jnp.float32)]
    pallas_call x0 -> x1, Pallas kernels: none -> 71.4 us  [step(): pl.pallas_call(functools.partial(kernel, n), out_shape=jax.ShapeDtypeStru...]
    dot_general x6 -> x0, matrix products: 43.2 us -> none  [the longest x2 31.7 us: einsum(): return jnp.einsum(form, a.astype(jnp.float32), b.astype(jnp.float32))]
    convert_element_type x4 -> x0, other arithmetic: 2.44 us -> none  [the longest x1 1.71 us: added(): (t.astype(jnp.float32) + lax.psum(term.astype(jnp.bfloat16), 'tp').astype...]
    reduce_sum x2 -> x0, other arithmetic: 2.33 us -> none  [normed(): scale = lax.rsqrt(jnp.mean(wide * wide, -1, keepdims=True) + 1e-06)]
  transfers between devices with their start and end apart: 2 -> 0, of which waited for: 2 -> 0; matrix products, arithmetic and copies ran while one was open for 0% -> 0% of each run, Pallas kernels for 0% -> 0%
where the time goes in v1:
time: 73.9 us; the launch traced here: 73.1 us
  Pallas kernels  71.4 us (97%)
  local copies, waits for them, and re-layouts  1.67 us (2%)
    pallas_call x1, Pallas kernels, step(): pl.pallas_call(functools.partial(kernel, n), out_shape=jax.ShapeDtypeStru...  71.4 us
    unnamed x1, local copies, waits for them, and re-layouts  1.67 us

profile of v1, /device:TPU:22, one launch (start us, length us, event | category | flops | bytes accessed | tf_op | source)
XLA Modules:
  0.0 73.1 jit_solution(7108530827555385682)
XLA Ops:
  0.0 71.4 %decoder_layer.1 = bf16[64,2048]{1,0:T(8,128)(2,1)} custom-call(bf16[64,2048]{1,0:T(8,128)(2,1)} %x_hbm.1, bf16[64,2048,128]{2,1,0:T(8,128)(2,1)} %bitcast.4, bf16[64,2048,128]{2,1,0:T(8,128)(2,1)} %bitcast.5, bf16[16,128]{1,0:T(8,128)(2,1)} %bitcast.6, bf16[2048,256]{1,0:T(8,128)(2,1)} %wq_hbm.1, bf16[256,2048]{1,0:T(8,128)(2,1)} %wo_hbm.1, ...), custom_call_target="tpu_custom_call" | custom-call | tf_op jit(solution)/shard_map/decoder_layer/pallas_call | solution.py:251
  71.4 1.7 %copy.13 = bf16[64,2048]{1,0:T(8,128)(2,1)} copy(bf16[64,2048]{1,0:T(8,128)(2,1)} %decoder_layer.1) | data formatting | bytes 524288

commit v2 on v0

v2 whole, which is shorter than its diff:
```python
import functools

import jax
import jax.numpy as jnp
import numpy as np
from jax import lax
from jax.experimental import pallas as pl
from jax.experimental.pallas import tpu as pltpu
from jax.sharding import PartitionSpec as P

HEAD = 128
THETA = 10000
F32, BF16 = jnp.float32, jnp.bfloat16

CH = 8
SLOTS = 3
LAG = 2
GROUP = 4
PASSES = (4, 3, 1)


def dot(a, b):
    return lax.dot_general(a, b, (((1,), (0,)), ((), ())), preferred_element_type=F32)


def dot_t(a, b):
    return lax.dot_general(a, b, (((1,), (1,)), ((), ())), preferred_element_type=F32)


def kernel(n, x_hbm, k_hbm, v_hbm, ga_hbm, wq_hbm, wo_hbm, gm_hbm, wg_hbm, wu_hbm, wd_hbm, cs_hbm, y_ref,
           xb, xf, ga, gm, cs, wq, wo, wg, wu, wd, kbuf, vbuf, qf, wbuf, pf, sbuf, rbuf, hbuf, bbuf, *rest):
    passes, (sem_in, sem_k, sem_v, rs_s, rs_r, ag_s, ag_r, rs2_s, rs2_r, ag2_s, ag2_r) = rest[:-11], rest[-11:]
    me = lax.axis_index("tp")
    rows, d = xb.shape
    chunks = rows // CH
    blk = d // n
    span = kbuf.shape[2] // 2

    far_first = sorted(range(1, n), key=lambda j: -min(j, n - j))

    def peer(j):
        return lax.rem(me + j, n)

    def load(i, src, dst):
        return pltpu.make_async_copy(src, dst, sem_in.at[i])

    first = [load(0, x_hbm, xb), load(1, ga_hbm, ga), load(2, cs_hbm, cs), load(3, wq_hbm, wq)]
    second = [load(4, wo_hbm, wo), load(5, gm_hbm, gm)]
    third = [load(6, wg_hbm, wg), load(7, wu_hbm, wu), load(8, wd_hbm, wd)]

    def fetch(hbm, buf, sem, c):
        slot = lax.rem(c, SLOTS)
        return pltpu.make_async_copy(hbm.at[pl.ds(c * CH, CH)], buf.at[slot], sem.at[slot])

    def fetch_k(c):
        return fetch(k_hbm, kbuf, sem_k, c)

    def fetch_v(c):
        return fetch(v_hbm, vbuf, sem_v, c)

    with jax.named_scope("start"):
        for cp in first:
            cp.start()
        fetch_k(0).start()
        barrier = pltpu.get_barrier_semaphore()
        for j in range(1, n):
            pl.semaphore_signal(barrier, inc=1, device_id={"tp": peer(j)})

    with jax.named_scope("wait_x"):
        for cp in first[:3]:
            cp.wait()
    with jax.named_scope("norm"):
        fetch_v(0).start()
        for cp in second:
            cp.start()
        fetch_k(1).start()
        xv = xb[...].astype(F32)
        xf[...] = xv
        scale = lax.rsqrt(jnp.sum(xv * xv, -1, keepdims=True) * (1.0 / d) + 1e-6)
        gav = ga[...].astype(F32)
        for i in range(d // 128):
            at = slice(128 * i, 128 * i + 128)
            bbuf[:, at] = (xf[:, at] * scale * gav[i:i + 1]).astype(BF16)
    with jax.named_scope("wait_wq"):
        first[3].wait()
        fetch_v(1).start()
    with jax.named_scope("qproj"):
        q = dot(bbuf[...], wq[...]).astype(BF16).astype(F32)
        for g in range(2):
            t = q[:, HEAD * g:HEAD * (g + 1)]
            turned = (t * cs[0:1] + pltpu.roll(t, HEAD // 2, 1) * cs[1:2]).astype(BF16).astype(F32)
            for i in range(rows // GROUP):
                qf[i, GROUP * g:GROUP * (g + 1)] = turned[GROUP * i:GROUP * (i + 1)]

    def rs_copy(c, j):
        return pltpu.make_async_remote_copy(
            src_ref=sbuf.at[c, peer(j)], dst_ref=rbuf.at[c, j - 1], send_sem=rs_s.at[c], recv_sem=rs_r.at[c],
            device_id={"tp": peer(j)})

    def ag_copy(c, j):
        return pltpu.make_async_remote_copy(
            src_ref=hbuf.at[c, me], dst_ref=hbuf.at[c, me], send_sem=ag_s.at[c], recv_sem=ag_r.at[c],
            device_id={"tp": peer(j)})

    def all_of(ref, sem):
        pltpu.make_async_copy(ref, ref, sem).wait()

    def finish(c):
        with jax.named_scope("finish_wait"):
            all_of(rbuf.at[c], rs_r.at[c])
        with jax.named_scope("finish"):
            total = pf[c, me]
            for j in range(n - 1):
                total = total + rbuf[c, j].astype(F32)
            total = total + xf[pl.ds(pl.multiple_of(c * CH, CH), CH), pl.ds(pl.multiple_of(me * blk, blk), blk)]
            hbuf[c, me] = total.astype(BF16)
            for j in far_first:
                ag_copy(c, j).start()

    tall = 4 * GROUP
    row = lax.broadcasted_iota(jnp.int32, (tall, 2 * HEAD), 0)
    row_w = lax.broadcasted_iota(jnp.int32, (tall, span), 0)
    col_w = lax.broadcasted_iota(jnp.int32, (tall, span), 1)
    own_head = (col_w % 2) == ((row_w // GROUP) % 2)
    groups = CH // GROUP

    def scored(c, g):
        slot = lax.rem(c, SLOTS)
        qg = qf[c * groups + g]
        zero = jnp.zeros_like(qg)
        base = jnp.concatenate([jnp.concatenate([qg, zero], 1), jnp.concatenate([zero, qg], 1)], 0)
        s = None
        for i in range(GROUP):
            lhs = jnp.where(row % GROUP == i, base, 0.0).astype(BF16)
            at = g * GROUP + i
            t = dot_t(lhs, jnp.concatenate([kbuf[slot, at, :span], kbuf[slot, at, span:]], 1))
            s = t if s is None else s + t
        return s

    def softmaxed(s):
        half = tall // 2
        s = jnp.where(own_head, s * HEAD**-0.5, -jnp.inf)
        m = jnp.max(s, -1, keepdims=True)
        m = jnp.maximum(m[:half], m[half:])
        e = jnp.exp(s - jnp.concatenate([m, m], 0))
        z = jnp.sum(e, -1, keepdims=True)
        z = 1.0 / (z[:half] + z[half:])
        return e * jnp.concatenate([z, z], 0)

    def mixed(c, g, w):
        slot = lax.rem(c, SLOTS)
        o = None
        for i in range(GROUP):
            lhs = jnp.where(row_w % GROUP == i, w, 0.0).astype(BF16)
            at = g * GROUP + i
            t = dot(lhs, jnp.concatenate([vbuf[slot, at, :span], vbuf[slot, at, span:]], 1))
            o = t if o is None else o + t
        return o[:tall // 2, :HEAD] + o[tall // 2:, HEAD:]

    def project(c, o):
        upper = lax.broadcasted_iota(jnp.int32, (CH, HEAD), 0) < GROUP
        head0 = jnp.where(upper, o[0], pltpu.roll(o[1], GROUP, 0))
        head1 = jnp.where(upper, pltpu.roll(o[0], GROUP, 0), o[1])
        seen = jnp.concatenate([head0, head1], 1).astype(BF16)
        term = dot(seen, wo[...])
        for j in range(n):
            part = term[:, blk * j:blk * (j + 1)]
            pf[c, j] = part
            sbuf[c, j] = part.astype(BF16)

    def send(c):
        for j in far_first:
            rs_copy(c, j).start()

    with jax.named_scope("k_wait"):
        fetch_k(0).wait()
        fetch_k(2).start()
    with jax.named_scope("weigh"):
        for g in range(groups):
            wbuf[g] = softmaxed(scored(0, g))
    with jax.named_scope("wait_wo"):
        for cp in second:
            cp.wait()
    with jax.named_scope("barrier_wait"):
        pl.semaphore_wait(barrier, n - 1)

    def attend(c, _):
        with jax.named_scope("k_wait"):
            fetch_k(c).wait()
        with jax.named_scope("v_wait"):
            fetch_v(c - 1).wait()

        @pl.when(c + 1 < chunks)
        def _():
            fetch_v(c + 1).start()

        @pl.when(c + 2 < chunks)
        def _():
            fetch_k(c + 2).start()

        @pl.when(c + 2 == chunks)
        def _():
            third[0].start()

        @pl.when(c + 1 == chunks)
        def _():
            third[1].start()

        with jax.named_scope("attend"):
            before = [wbuf[g] for g in range(groups)]
            scores = [scored(c, g) for g in range(groups)]
            o = [mixed(c - 1, g, before[g]) for g in range(groups)]
            for g in range(groups):
                wbuf[g] = softmaxed(scores[g])
            project(c - 1, o)
        with jax.named_scope("send"):
            send(c - 1)

        @pl.when(c - 1 >= LAG)
        def _():
            finish(c - 1 - LAG)

        return 0

    lax.fori_loop(1, chunks, attend, 0)
    with jax.named_scope("v_wait"):
        fetch_v(chunks - 1).wait()
    third[2].start()
    with jax.named_scope("mix"):
        project(chunks - 1, [mixed(chunks - 1, g, wbuf[g]) for g in range(groups)])
    with jax.named_scope("send"):
        send(chunks - 1)
    for c in range(chunks - 1 - LAG, chunks - 1):
        finish(c)

    gmv = gm[...].astype(F32)

    def rs2_copy(p, j):
        return pltpu.make_async_remote_copy(
            src_ref=passes[4 * p + 1].at[peer(j)], dst_ref=passes[4 * p + 2].at[j - 1], send_sem=rs2_s.at[p],
            recv_sem=rs2_r.at[p], device_id={"tp": peer(j)})

    def ag2_copy(p, j):
        ybuf = passes[4 * p + 3]
        return pltpu.make_async_remote_copy(
            src_ref=ybuf.at[me], dst_ref=ybuf.at[me], send_sem=ag2_s.at[p], recv_sem=ag2_r.at[p],
            device_id={"tp": peer(j)})

    def feed(p, lo, hi, between=None):
        p2, s2 = passes[4 * p:4 * p + 2]
        count = (hi - lo) * CH
        with jax.named_scope("ag_wait"):
            for c in range(lo, hi):
                all_of(rbuf.at[c], ag_r.at[c])

        def h_block(j):
            return hbuf[lo:hi, j].astype(F32).reshape(count, blk)

        with jax.named_scope("feed"):
            total = None
            for j in range(n):
                hj = h_block(j)
                t = jnp.sum(hj * hj, -1, keepdims=True)
                total = t if total is None else total + t
            scale = lax.rsqrt(total * (1.0 / d) + 1e-6)
            at_rows = slice(lo * CH, hi * CH)
            for j in range(n):
                hj = h_block(j)
                for i in range(blk // 128):
                    g = j * (blk // 128) + i
                    bbuf[at_rows, 128 * g:128 * g + 128] = (hj[:, 128 * i:128 * i + 128] * scale * gmv[g:g + 1]).astype(BF16)
        if p == 0:
            with jax.named_scope("w_wait"):
                for cp in third:
                    cp.wait()
        with jax.named_scope("mlp"):
            hidden = []
            for f in range(wg.shape[1] // 256):
                at = slice(256 * f, 256 * f + 256)
                gate = dot(bbuf[at_rows, :], wg[:, at])
                up = dot(bbuf[at_rows, :], wu[:, at])
                hidden.append((jax.nn.silu(gate) * up).astype(BF16))
            hidden = jnp.concatenate(hidden, 1)
        if between is not None:
            between()
        with jax.named_scope("down"):
            for j in range(n):
                part = dot(hidden, wd[:, blk * j:blk * (j + 1)])
                p2[j] = part
                s2[j] = part.astype(BF16)
        with jax.named_scope("send2"):
            for j in far_first:
                rs2_copy(p, j).start()

    def finish2(p, lo, hi):
        p2, _, r2, ybuf = passes[4 * p:4 * p + 4]
        with jax.named_scope("rs2_wait"):
            all_of(r2, rs2_r.at[p])
        with jax.named_scope("sum2"):
            total = p2[me]
            for j in range(n - 1):
                total = total + r2[j].astype(F32)
            total = total + hbuf[lo:hi, me].astype(F32).reshape((hi - lo) * CH, blk)
            ybuf[me] = total.astype(BF16)
            for j in far_first:
                ag2_copy(p, j).start()

    def close(p, lo, hi):
        _, _, r2, ybuf = passes[4 * p:4 * p + 4]
        with jax.named_scope("ag2_wait"):
            all_of(r2, ag2_r.at[p])
        with jax.named_scope("out"):
            for j in range(n):
                y_ref[lo * CH:hi * CH, blk * j:blk * (j + 1)] = ybuf[j]

    ends = [sum(PASSES[:p + 1]) for p in range(len(PASSES))]
    parts = [(hi - count, hi) for hi, count in zip(ends, PASSES)]
    for p, (lo, hi) in enumerate(parts):
        feed(p, lo, hi, functools.partial(finish, chunks - 1) if p == 0 else None)
    for p, (lo, hi) in enumerate(parts):
        finish2(p, lo, hi)
    with jax.named_scope("sends_wait"):
        for c in range(chunks):
            all_of(rbuf.at[c], rs_s.at[c])
            all_of(rbuf.at[c], ag_s.at[c])
    for p, (lo, hi) in enumerate(parts):
        close(p, lo, hi)
    for p in range(len(PASSES)):
        r2 = passes[4 * p + 2]
        all_of(r2, rs2_s.at[p])
        all_of(r2, ag2_s.at[p])


def solution(mesh):
    n = mesh.shape["tp"]

    def step(x, k_cache, v_cache, gain_a, wq, wo, gain_m, w_gate, w_up, w_down):
        rows, d = x.shape
        batch, cache, heads, head = k_cache.shape
        ff = w_gate.shape[1]
        chunks, blk = rows // CH, d // n
        half = head // 2
        angle = (cache - 1) * float(THETA) ** (-np.arange(half) / half)
        cos, sin = np.cos(angle), np.sin(angle)
        cs = np.zeros((8, head), np.float32)
        cs[0], cs[1] = np.concatenate([cos, cos]), np.concatenate([-sin, sin])
        keys = k_cache.reshape(batch, cache * heads, head)
        values = v_cache.reshape(batch, cache * heads, head)
        second_half = []
        assert sum(PASSES) == chunks
        for count in (CH * p for p in PASSES):
            second_half += [
                pltpu.VMEM((n, count, blk), F32),
                pltpu.VMEM((n, count, blk), BF16),
                pltpu.VMEM((n - 1, count, blk), BF16),
                pltpu.VMEM((n, count, blk), BF16),
            ]
        dma = pltpu.SemaphoreType.DMA
        return pl.pallas_call(
            functools.partial(kernel, n),
            out_shape=jax.ShapeDtypeStruct((rows, d), BF16),
            in_specs=[pl.BlockSpec(memory_space=pl.ANY)] * 11,
            out_specs=pl.BlockSpec(memory_space=pltpu.VMEM),
            scratch_shapes=[
                pltpu.VMEM((rows, d), BF16),
                pltpu.VMEM((rows, d), F32),
                pltpu.VMEM((d // 128, 128), BF16),
                pltpu.VMEM((d // 128, 128), BF16),
                pltpu.VMEM((8, head), F32),
                pltpu.VMEM(wq.shape, BF16),
                pltpu.VMEM(wo.shape, BF16),
                pltpu.VMEM(w_gate.shape, BF16),
                pltpu.VMEM(w_up.shape, BF16),
                pltpu.VMEM(w_down.shape, BF16),
                pltpu.VMEM((SLOTS, CH, cache * heads, head), BF16),
                pltpu.VMEM((SLOTS, CH, cache * heads, head), BF16),
                pltpu.VMEM((rows // GROUP, heads * GROUP, head), F32),
                pltpu.VMEM((CH // GROUP, 4 * GROUP, cache * heads // 2), F32),
                pltpu.VMEM((chunks, n, CH, blk), F32),
                pltpu.VMEM((chunks, n, CH, blk), BF16),
                pltpu.VMEM((chunks, n - 1, CH, blk), BF16),
                pltpu.VMEM((chunks, n, CH, blk), BF16),
                pltpu.VMEM((rows, d), BF16),
                *second_half,
                dma((9,)), dma((SLOTS,)), dma((SLOTS,)),
                dma((chunks,)), dma((chunks,)), dma((chunks,)), dma((chunks,)),
                *[dma((len(PASSES),))] * 4,
            ],
            compiler_params=pltpu.CompilerParams(
                collective_id=0, has_side_effects=True, vmem_limit_bytes=64 * 1024 * 1024 - 65536),
            name="decoder_layer",
        )(x, keys, values, gain_a.reshape(d // 128, 128), wq, wo, gain_m.reshape(d // 128, 128), w_gate, w_up, w_down, jnp.asarray(cs))

    states, cache, columns, rows_of = P("dp", None), P("dp", None, "tp", None), P(None, "tp"), P("tp", None)
    return jax.shard_map(
        step,
        mesh=mesh,
        in_specs=(states, cache, cache, P(None), columns, rows_of, P(None), columns, columns, rows_of),
        out_specs=states,
        check_vma=False,
    )
```

time: 198 us -> 53.1 us (0.27)
  waiting for transfers between devices: 135 us -> 0 us
  Pallas kernels: 0 us -> 51.1 us
  matrix products: 43.2 us -> 0 us
  between operations: 13.5 us -> 0.01 us
  other arithmetic: 5.44 us -> 0 us
    psum x2 -> x0, waiting for transfers between devices: 135 us -> none  [added(): lax.psum(term.astype(jnp.bfloat16), 'tp').astype(jnp.float32)]
    pallas_call x0 -> x1, Pallas kernels: none -> 51.1 us  [step(): pl.pallas_call(functools.partial(kernel, n), out_shape=jax.ShapeDtypeStru...]
    dot_general x6 -> x0, matrix products: 43.2 us -> none  [the longest x2 31.7 us: einsum(): return jnp.einsum(form, a.astype(jnp.float32), b.astype(jnp.float32))]
    convert_element_type x4 -> x0, other arithmetic: 2.44 us -> none  [the longest x1 1.71 us: added(): (t.astype(jnp.float32) + lax.psum(term.astype(jnp.bfloat16), 'tp').astype...]
    reduce_sum x2 -> x0, other arithmetic: 2.33 us -> none  [normed(): scale = lax.rsqrt(jnp.mean(wide * wide, -1, keepdims=True) + 1e-06)]
  transfers between devices with their start and end apart: 2 -> 0, of which waited for: 2 -> 0; matrix products, arithmetic and copies ran while one was open for 0% -> 0% of each run, Pallas kernels for 0% -> 0%
where the time goes in v2:
time: 53.1 us; the launch traced here: 52.8 us
  Pallas kernels  51.1 us (96%)
  local copies, waits for them, and re-layouts  1.67 us (3%)
    pallas_call x1, Pallas kernels, step(): pl.pallas_call(functools.partial(kernel, n), out_shape=jax.ShapeDtypeStru...  51.1 us
    unnamed x1, local copies, waits for them, and re-layouts  1.67 us

profile of v2, /device:TPU:22, one launch (start us, length us, event | category | flops | bytes accessed | tf_op | source)
XLA Modules:
  0.0 52.8 jit_solution(7962849600933452357)
XLA Ops:
  0.0 51.1 %decoder_layer.1 = bf16[64,2048]{1,0:T(8,128)(2,1)} custom-call(bf16[64,2048]{1,0:T(8,128)(2,1)} %x_hbm.1, bf16[64,2048,128]{2,1,0:T(8,128)(2,1)} %bitcast.4, bf16[64,2048,128]{2,1,0:T(8,128)(2,1)} %bitcast.5, bf16[16,128]{1,0:T(8,128)(2,1)} %bitcast.6, bf16[2048,256]{1,0:T(8,128)(2,1)} %wq_hbm.1, bf16[256,2048]{1,0:T(8,128)(2,1)} %wo_hbm.1, ...), custom_call_target="tpu_custom_call" | custom-call | tf_op jit(solution)/shard_map/decoder_layer/pallas_call | solution.py:359
  51.1 1.7 %copy.13 = bf16[64,2048]{1,0:T(8,128)(2,1)} copy(bf16[64,2048]{1,0:T(8,128)(2,1)} %decoder_layer.1) | data formatting | bytes 524288

commit v3 on v2

--- a/solution.py
+++ b/solution.py
@@ -14,9 +14,10 @@
 
 CH = 8
 SLOTS = 3
+AHEAD = 2
 LAG = 2
 GROUP = 4
-PASSES = (4, 3, 1)
+PASSES = (2, 2, 2, 2)
 
 
 def dot(a, b):
@@ -46,17 +47,31 @@
 
     first = [load(0, x_hbm, xb), load(1, ga_hbm, ga), load(2, cs_hbm, cs), load(3, wq_hbm, wq)]
     second = [load(4, wo_hbm, wo), load(5, gm_hbm, gm)]
-    third = [load(6, wg_hbm, wg), load(7, wu_hbm, wu), load(8, wd_hbm, wd)]
-
-    def fetch(hbm, buf, sem, c):
-        slot = lax.rem(c, SLOTS)
-        return pltpu.make_async_copy(hbm.at[pl.ds(c * CH, CH)], buf.at[slot], sem.at[slot])
+
+    def load_part(i, src, dst, part):
+        at = pl.ds(part * (src.shape[0] // 2), src.shape[0] // 2)
+        return pltpu.make_async_copy(src.at[at], dst.at[at], sem_in.at[i])
+
+    third = [load_part(6 + 2 * i + part, src, dst, part)
+             for i, (src, dst) in enumerate(((wg_hbm, wg), (wu_hbm, wu), (wd_hbm, wd))) for part in range(2)]
+
+    class Fetch:
+        def __init__(self, hbm, buf, sem, c):
+            self.hbm, self.c, slot = hbm, c, lax.rem(c, SLOTS)
+            self.buf, self.sem = buf.at[slot], sem.at[slot]
+
+        def start(self):
+            for g in range(0, CH, GROUP):
+                pltpu.make_async_copy(self.hbm.at[pl.ds(self.c * CH + g, GROUP)], self.buf.at[pl.ds(g, GROUP)], self.sem).start()
+
+        def wait(self):
+            pltpu.make_async_copy(self.hbm.at[pl.ds(self.c * CH, CH)], self.buf, self.sem).wait()
 
     def fetch_k(c):
-        return fetch(k_hbm, kbuf, sem_k, c)
+        return Fetch(k_hbm, kbuf, sem_k, c)
 
     def fetch_v(c):
-        return fetch(v_hbm, vbuf, sem_v, c)
+        return Fetch(v_hbm, vbuf, sem_v, c)
 
     with jax.named_scope("start"):
         for cp in first:
@@ -70,10 +85,8 @@
         for cp in first[:3]:
             cp.wait()
     with jax.named_scope("norm"):
+        fetch_k(1).start()
         fetch_v(0).start()
-        for cp in second:
-            cp.start()
-        fetch_k(1).start()
         xv = xb[...].astype(F32)
         xf[...] = xv
         scale = lax.rsqrt(jnp.sum(xv * xv, -1, keepdims=True) * (1.0 / d) + 1e-6)
@@ -83,7 +96,9 @@
             bbuf[:, at] = (xf[:, at] * scale * gav[i:i + 1]).astype(BF16)
     with jax.named_scope("wait_wq"):
         first[3].wait()
-        fetch_v(1).start()
+        for cp in second:
+            cp.start()
+        fetch_k(2).start()
     with jax.named_scope("qproj"):
         q = dot(bbuf[...], wq[...]).astype(BF16).astype(F32)
         for g in range(2):
@@ -172,12 +187,15 @@
         for j in far_first:
             rs_copy(c, j).start()
 
-    with jax.named_scope("k_wait"):
-        fetch_k(0).wait()
-        fetch_k(2).start()
-    with jax.named_scope("weigh"):
-        for g in range(groups):
-            wbuf[g] = softmaxed(scored(0, g))
+    for c in range(AHEAD):
+        with jax.named_scope("k_wait"):
+            fetch_k(c).wait()
+        with jax.named_scope("weigh"):
+            for g in range(groups):
+                wbuf[c, g] = softmaxed(scored(c, g))
+        if c + 1 < AHEAD:
+            fetch_v(c + 1).start()
+            fetch_k(c + SLOTS).start()
     with jax.named_scope("wait_wo"):
         for cp in second:
             cp.wait()
@@ -185,54 +203,56 @@
         pl.semaphore_wait(barrier, n - 1)
 
     def attend(c, _):
+        ready = c - AHEAD
         with jax.named_scope("k_wait"):
             fetch_k(c).wait()
         with jax.named_scope("v_wait"):
-            fetch_v(c - 1).wait()
-
-        @pl.when(c + 1 < chunks)
-        def _():
-            fetch_v(c + 1).start()
+            fetch_v(ready).wait()
+        fetch_v(c).start()
 
         @pl.when(c + 2 < chunks)
         def _():
             fetch_k(c + 2).start()
 
-        @pl.when(c + 2 == chunks)
+        @pl.when(c + 1 == chunks)
         def _():
             third[0].start()
 
-        @pl.when(c + 1 == chunks)
+        with jax.named_scope("attend"):
+            at = lax.rem(c, AHEAD)
+            before = [wbuf[at, g] for g in range(groups)]
+            scores = [scored(c, g) for g in range(groups)]
+            o = [mixed(ready, g, before[g]) for g in range(groups)]
+            for g in range(groups):
+                wbuf[at, g] = softmaxed(scores[g])
+            project(ready, o)
+        with jax.named_scope("send"):
+            send(ready)
+
+        @pl.when(ready >= LAG)
         def _():
-            third[1].start()
-
-        with jax.named_scope("attend"):
-            before = [wbuf[g] for g in range(groups)]
-            scores = [scored(c, g) for g in range(groups)]
-            o = [mixed(c - 1, g, before[g]) for g in range(groups)]
-            for g in range(groups):
-                wbuf[g] = softmaxed(scores[g])
-            project(c - 1, o)
-        with jax.named_scope("send"):
-            send(c - 1)
-
-        @pl.when(c - 1 >= LAG)
-        def _():
-            finish(c - 1 - LAG)
+            finish(ready - LAG)
 
         return 0
 
-    lax.fori_loop(1, chunks, attend, 0)
+    lax.fori_loop(AHEAD, chunks, attend, 0)
+    for cp in third[1:]:
+        cp.start()
+    rest_of = range(chunks - AHEAD, chunks)
     with jax.named_scope("v_wait"):
-        fetch_v(chunks - 1).wait()
-    third[2].start()
+        for c in rest_of:
+            fetch_v(c).wait()
     with jax.named_scope("mix"):
-        project(chunks - 1, [mixed(chunks - 1, g, wbuf[g]) for g in range(groups)])
+        o = [[mixed(c, g, wbuf[c % AHEAD, g]) for g in range(groups)] for c in rest_of]
+        for c in rest_of:
+            project(c, o[c - rest_of[0]])
     with jax.named_scope("send"):
-        send(chunks - 1)
-    for c in range(chunks - 1 - LAG, chunks - 1):
-        finish(c)
-
+        for c in rest_of:
+            send(c)
+    finish(chunks - 4)
+
+    ends = [sum(PASSES[:p + 1]) for p in range(len(PASSES))]
+    parts = [(hi - count, hi) for hi, count in zip(ends, PASSES)]
     gmv = gm[...].astype(F32)
 
     def rs2_copy(p, j):
@@ -240,10 +260,13 @@
             src_ref=passes[4 * p + 1].at[peer(j)], dst_ref=passes[4 * p + 2].at[j - 1], send_sem=rs2_s.at[p],
             recv_sem=rs2_r.at[p], device_id={"tp": peer(j)})
 
+    def own_part(p):
+        lo, hi = parts[p]
+        return y_ref.at[pl.ds(lo * CH, (hi - lo) * CH), pl.ds(pl.multiple_of(me * blk, blk), blk)]
+
     def ag2_copy(p, j):
-        ybuf = passes[4 * p + 3]
         return pltpu.make_async_remote_copy(
-            src_ref=ybuf.at[me], dst_ref=ybuf.at[me], send_sem=ag2_s.at[p], recv_sem=ag2_r.at[p],
+            src_ref=passes[4 * p + 3], dst_ref=own_part(p), send_sem=ag2_s.at[p], recv_sem=ag2_r.at[p],
             device_id={"tp": peer(j)})
 
     def feed(p, lo, hi, between=None):
@@ -271,7 +294,7 @@
                     bbuf[at_rows, 128 * g:128 * g + 128] = (hj[:, 128 * i:128 * i + 128] * scale * gmv[g:g + 1]).astype(BF16)
         if p == 0:
             with jax.named_scope("w_wait"):
-                for cp in third:
+                for cp in third[:4]:
                     cp.wait()
         with jax.named_scope("mlp"):
             hidden = []
@@ -282,7 +305,11 @@
                 hidden.append((jax.nn.silu(gate) * up).astype(BF16))
             hidden = jnp.concatenate(hidden, 1)
         if between is not None:
-            between()
+            finish(between)
+        if p == 0:
+            with jax.named_scope("w_wait"):
+                for cp in third[4:]:
+                    cp.wait()
         with jax.named_scope("down"):
             for j in range(n):
                 part = dot(hidden, wd[:, blk * j:blk * (j + 1)])
@@ -301,34 +328,37 @@
             for j in range(n - 1):
                 total = total + r2[j].astype(F32)
             total = total + hbuf[lo:hi, me].astype(F32).reshape((hi - lo) * CH, blk)
-            ybuf[me] = total.astype(BF16)
+            ybuf[...] = total.astype(BF16)
+            own_part(p)[...] = ybuf[...]
             for j in far_first:
                 ag2_copy(p, j).start()
 
-    def close(p, lo, hi):
-        _, _, r2, ybuf = passes[4 * p:4 * p + 4]
-        with jax.named_scope("ag2_wait"):
-            all_of(r2, ag2_r.at[p])
-        with jax.named_scope("out"):
-            for j in range(n):
-                y_ref[lo * CH:hi * CH, blk * j:blk * (j + 1)] = ybuf[j]
-
-    ends = [sum(PASSES[:p + 1]) for p in range(len(PASSES))]
-    parts = [(hi - count, hi) for hi, count in zip(ends, PASSES)]
+    last = len(parts) - 1
     for p, (lo, hi) in enumerate(parts):
-        feed(p, lo, hi, functools.partial(finish, chunks - 1) if p == 0 else None)
-    for p, (lo, hi) in enumerate(parts):
+        if p == last:
+            finish2(0, *parts[0])
+        feed(p, lo, hi, chunks - 3 if p == 0 else None)
+        if p == 0:
+            finish(chunks - 2)
+            finish(chunks - 1)
+    for p, (lo, hi) in enumerate(parts[1:], 1):
         finish2(p, lo, hi)
     with jax.named_scope("sends_wait"):
         for c in range(chunks):
             all_of(rbuf.at[c], rs_s.at[c])
             all_of(rbuf.at[c], ag_s.at[c])
-    for p, (lo, hi) in enumerate(parts):
-        close(p, lo, hi)
     for p in range(len(PASSES)):
         r2 = passes[4 * p + 2]
         all_of(r2, rs2_s.at[p])
         all_of(r2, ag2_s.at[p])
+        with jax.named_scope("ag2_wait"):
+            all_of(r2, ag2_r.at[p])
+
+
+def put_out(y_ref, out_ref, sem):
+    copy = pltpu.make_async_copy(y_ref, out_ref, sem)
+    copy.start()
+    copy.wait()
 
 
 def solution(mesh):
@@ -353,12 +383,12 @@
                 pltpu.VMEM((n, count, blk), F32),
                 pltpu.VMEM((n, count, blk), BF16),
                 pltpu.VMEM((n - 1, count, blk), BF16),
-                pltpu.VMEM((n, count, blk), BF16),
+                pltpu.VMEM((count, blk), BF16),
             ]
         dma = pltpu.SemaphoreType.DMA
-        return pl.pallas_call(
+        y = pl.pallas_call(
             functools.partial(kernel, n),
-            out_shape=jax.ShapeDtypeStruct((rows, d), BF16),
+            out_shape=pltpu.VMEM((rows, d), BF16),
             in_specs=[pl.BlockSpec(memory_space=pl.ANY)] * 11,
             out_specs=pl.BlockSpec(memory_space=pltpu.VMEM),
             scratch_shapes=[
@@ -375,21 +405,30 @@
                 pltpu.VMEM((SLOTS, CH, cache * heads, head), BF16),
                 pltpu.VMEM((SLOTS, CH, cache * heads, head), BF16),
                 pltpu.VMEM((rows // GROUP, heads * GROUP, head), F32),
-                pltpu.VMEM((CH // GROUP, 4 * GROUP, cache * heads // 2), F32),
+                pltpu.VMEM((AHEAD, CH // GROUP, 4 * GROUP, cache * heads // 2), F32),
                 pltpu.VMEM((chunks, n, CH, blk), F32),
                 pltpu.VMEM((chunks, n, CH, blk), BF16),
                 pltpu.VMEM((chunks, n - 1, CH, blk), BF16),
                 pltpu.VMEM((chunks, n, CH, blk), BF16),
                 pltpu.VMEM((rows, d), BF16),
                 *second_half,
-                dma((9,)), dma((SLOTS,)), dma((SLOTS,)),
+                dma((12,)), dma((SLOTS,)), dma((SLOTS,)),
                 dma((chunks,)), dma((chunks,)), dma((chunks,)), dma((chunks,)),
                 *[dma((len(PASSES),))] * 4,
             ],
             compiler_params=pltpu.CompilerParams(
-                collective_id=0, has_side_effects=True, vmem_limit_bytes=64 * 1024 * 1024 - 65536),
+                collective_id=0, has_side_effects=True, vmem_limit_bytes=64336 * 1024),
             name="decoder_layer",
         )(x, keys, values, gain_a.reshape(d // 128, 128), wq, wo, gain_m.reshape(d // 128, 128), w_gate, w_up, w_down, jnp.asarray(cs))
+        return pl.pallas_call(
+            put_out,
+            out_shape=jax.ShapeDtypeStruct((rows, d), BF16),
+            in_specs=[pl.BlockSpec(memory_space=pltpu.VMEM)],
+            out_specs=pl.BlockSpec(memory_space=pl.ANY),
+            scratch_shapes=[dma(())],
+            compiler_params=pltpu.CompilerParams(vmem_limit_bytes=1024 * 1024),
+            name="put_out",
+        )(y)
 
     states, cache, columns, rows_of = P("dp", None), P("dp", None, "tp", None), P(None, "tp"), P("tp", None)
     return jax.shard_map(

time: 53.1 us -> 51.2 us (0.964)
  local copies, waits for them, and re-layouts: 1.67 us -> 0 us
    unnamed x1 -> x0, local copies, waits for them, and re-layouts: 1.67 us -> none
    pallas_call x1 -> x2, Pallas kernels: 51.1 us -> 51.1 us  [the longest x1 50.4 us: step(): pl.pallas_call(functools.partial(kernel, n), out_shape=pltpu.VMEM((rows,...]
where the time goes in v3:
time: 51.2 us; the launch traced here: 51.1 us
  Pallas kernels  51.1 us (100%)
    pallas_call x1, Pallas kernels, step(): pl.pallas_call(functools.partial(kernel, n), out_shape=pltpu.VMEM((rows,...  50.4 us

profile of v3, /device:TPU:22, one launch (start us, length us, event | category | flops | bytes accessed | tf_op | source)
XLA Modules:
  0.0 51.1 jit_solution(9487796417678686464)
XLA Ops:
  0.0 50.4 %decoder_layer.1.y_ref = bf16[64,2048]{1,0:T(8,128)(2,1)S(1)} custom-call(bf16[64,2048]{1,0:T(8,128)(2,1)} %x_hbm.1, bf16[64,2048,128]{2,1,0:T(8,128)(2,1)} %bitcast.4, bf16[64,2048,128]{2,1,0:T(8,128)(2,1)} %bitcast.5, bf16[16,128]{1,0:T(8,128)(2,1)} %bitcast.6, bf16[2048,256]{1,0:T(8,128)(2,1)} %wq_hbm.1, bf16[256,2048]{1,0:T(8,128)(2,1)} %wo_hbm.1, ...), custom_call_target="tpu_custom_call" | custom-call | tf_op jit(solution)/shard_map/decoder_layer/pallas_call | solution.py:389
  50.4 0.7 %put_out.1 = bf16[64,2048]{1,0:T(8,128)(2,1)} custom-call(bf16[64,2048]{1,0:T(8,128)(2,1)S(1)} %decoder_layer.1.y_ref), custom_call_target="tpu_custom_call" | custom-call | tf_op jit(solution)/shard_map/put_out/pallas_call | solution.py:423

commit v4 on v3

--- a/solution.py
+++ b/solution.py
@@ -14,10 +14,10 @@
 
 CH = 8
 SLOTS = 3
-AHEAD = 2
+AHEAD = 1
 LAG = 2
 GROUP = 4
-PASSES = (2, 2, 2, 2)
+PASSES = (4, 2, 2)
 
 
 def dot(a, b):
@@ -85,8 +85,8 @@
         for cp in first[:3]:
             cp.wait()
     with jax.named_scope("norm"):
+        fetch_v(0).start()
         fetch_k(1).start()
-        fetch_v(0).start()
         xv = xb[...].astype(F32)
         xf[...] = xv
         scale = lax.rsqrt(jnp.sum(xv * xv, -1, keepdims=True) * (1.0 / d) + 1e-6)
@@ -98,7 +98,7 @@
         first[3].wait()
         for cp in second:
             cp.start()
-        fetch_k(2).start()
+        fetch_v(1).start()
     with jax.named_scope("qproj"):
         q = dot(bbuf[...], wq[...]).astype(BF16).astype(F32)
         for g in range(2):
@@ -187,15 +187,12 @@
         for j in far_first:
             rs_copy(c, j).start()
 
-    for c in range(AHEAD):
-        with jax.named_scope("k_wait"):
-            fetch_k(c).wait()
-        with jax.named_scope("weigh"):
-            for g in range(groups):
-                wbuf[c, g] = softmaxed(scored(c, g))
-        if c + 1 < AHEAD:
-            fetch_v(c + 1).start()
-            fetch_k(c + SLOTS).start()
+    with jax.named_scope("k_wait"):
+        fetch_k(0).wait()
+        fetch_k(2).start()
+    with jax.named_scope("weigh"):
+        for g in range(groups):
+            wbuf[0, g] = softmaxed(scored(0, g))
     with jax.named_scope("wait_wo"):
         for cp in second:
             cp.wait()
@@ -208,7 +205,10 @@
             fetch_k(c).wait()
         with jax.named_scope("v_wait"):
             fetch_v(ready).wait()
-        fetch_v(c).start()
+
+        @pl.when(c + 1 < chunks)
+        def _():
+            fetch_v(c + 1).start()
 
         @pl.when(c + 2 < chunks)
         def _():
@@ -216,7 +216,8 @@
 
         @pl.when(c + 1 == chunks)
         def _():
-            third[0].start()
+            for cp in third[:4]:
+                cp.start()
 
         with jax.named_scope("attend"):
             at = lax.rem(c, AHEAD)
@@ -236,12 +237,12 @@
         return 0
 
     lax.fori_loop(AHEAD, chunks, attend, 0)
-    for cp in third[1:]:
-        cp.start()
     rest_of = range(chunks - AHEAD, chunks)
     with jax.named_scope("v_wait"):
         for c in rest_of:
             fetch_v(c).wait()
+        for cp in third[4:]:
+            cp.start()
     with jax.named_scope("mix"):
         o = [[mixed(c, g, wbuf[c % AHEAD, g]) for g in range(groups)] for c in rest_of]
         for c in rest_of:
@@ -249,7 +250,7 @@
     with jax.named_scope("send"):
         for c in rest_of:
             send(c)
-    finish(chunks - 4)
+    finish(chunks - 3)
 
     ends = [sum(PASSES[:p + 1]) for p in range(len(PASSES))]
     parts = [(hi - count, hi) for hi, count in zip(ends, PASSES)]
@@ -269,7 +270,7 @@
             src_ref=passes[4 * p + 3], dst_ref=own_part(p), send_sem=ag2_s.at[p], recv_sem=ag2_r.at[p],
             device_id={"tp": peer(j)})
 
-    def feed(p, lo, hi, between=None):
+    def feed(p, lo, hi, between=None, after=()):
         p2, s2 = passes[4 * p:4 * p + 2]
         count = (hi - lo) * CH
         with jax.named_scope("ag_wait"):
@@ -315,6 +316,8 @@
                 part = dot(hidden, wd[:, blk * j:blk * (j + 1)])
                 p2[j] = part
                 s2[j] = part.astype(BF16)
+        for c in after:
+            finish(c)
         with jax.named_scope("send2"):
             for j in far_first:
                 rs2_copy(p, j).start()
@@ -333,15 +336,12 @@
             for j in far_first:
                 ag2_copy(p, j).start()
 
-    last = len(parts) - 1
     for p, (lo, hi) in enumerate(parts):
-        if p == last:
-            finish2(0, *parts[0])
-        feed(p, lo, hi, chunks - 3 if p == 0 else None)
         if p == 0:
-            finish(chunks - 2)
-            finish(chunks - 1)
-    for p, (lo, hi) in enumerate(parts[1:], 1):
+            feed(p, lo, hi, None, (chunks - 2, chunks - 1))
+        else:
+            feed(p, lo, hi)
+    for p, (lo, hi) in enumerate(parts):
         finish2(p, lo, hi)
     with jax.named_scope("sends_wait"):
         for c in range(chunks):

time: 51.2 us -> 50.2 us (0.980)
  Pallas kernels: 51.1 us -> 50 us
    pallas_call x1, Pallas kernels: 50.4 us -> 49.3 us  [step(): pl.pallas_call(functools.partial(kernel, n), out_shape=pltpu.VMEM((rows,...]
where the time goes in v4:
time: 50.2 us; the launch traced here: 50 us
  Pallas kernels  50 us (100%)
    pallas_call x1, Pallas kernels, step(): pl.pallas_call(functools.partial(kernel, n), out_shape=pltpu.VMEM((rows,...  49.3 us

profile of v4, /device:TPU:22, one launch (start us, length us, event | category | flops | bytes accessed | tf_op | source)
XLA Modules:
  0.0 50.0 jit_solution(15592240280117293712)
XLA Ops:
  0.0 49.3 %decoder_layer.1.y_ref = bf16[64,2048]{1,0:T(8,128)(2,1)S(1)} custom-call(bf16[64,2048]{1,0:T(8,128)(2,1)} %x_hbm.1, bf16[64,2048,128]{2,1,0:T(8,128)(2,1)} %bitcast.4, bf16[64,2048,128]{2,1,0:T(8,128)(2,1)} %bitcast.5, bf16[16,128]{1,0:T(8,128)(2,1)} %bitcast.6, bf16[2048,256]{1,0:T(8,128)(2,1)} %wq_hbm.1, bf16[256,2048]{1,0:T(8,128)(2,1)} %wo_hbm.1, ...), custom_call_target="tpu_custom_call" | custom-call | tf_op jit(solution)/shard_map/decoder_layer/pallas_call | solution.py:389
  49.3 0.7 %put_out.1 = bf16[64,2048]{1,0:T(8,128)(2,1)} custom-call(bf16[64,2048]{1,0:T(8,128)(2,1)S(1)} %decoder_layer.1.y_ref), custom_call_target="tpu_custom_call" | custom-call | tf_op jit(solution)/shard_map/put_out/pallas_call | solution.py:423

commit v5 on v4

--- a/solution.py
+++ b/solution.py
@@ -42,18 +42,24 @@
     def peer(j):
         return lax.rem(me + j, n)
 
-    def load(i, src, dst):
-        return pltpu.make_async_copy(src, dst, sem_in.at[i])
-
-    first = [load(0, x_hbm, xb), load(1, ga_hbm, ga), load(2, cs_hbm, cs), load(3, wq_hbm, wq)]
-    second = [load(4, wo_hbm, wo), load(5, gm_hbm, gm)]
-
-    def load_part(i, src, dst, part):
-        at = pl.ds(part * (src.shape[0] // 2), src.shape[0] // 2)
-        return pltpu.make_async_copy(src.at[at], dst.at[at], sem_in.at[i])
-
-    third = [load_part(6 + 2 * i + part, src, dst, part)
-             for i, (src, dst) in enumerate(((wg_hbm, wg), (wu_hbm, wu), (wd_hbm, wd))) for part in range(2)]
+    copy = pltpu.make_async_copy
+    first = [copy(x_hbm, xb, sem_v.at[1]), copy(ga_hbm, ga, sem_v.at[2]), copy(cs_hbm, cs, sem_k.at[1]), copy(wq_hbm, wq, sem_k.at[2])]
+    second = [copy(wo_hbm, wo, sem_in), copy(gm_hbm, gm, sem_v.at[2])]
+
+    class Halves:
+        def __init__(self, src, dst, sem):
+            self.src, self.dst, self.sem = src, dst, sem
+
+        def start(self):
+            half = self.src.shape[0] // 2
+            for part in range(2):
+                at = pl.ds(part * half, half)
+                copy(self.src.at[at], self.dst.at[at], self.sem).start()
+
+        def wait(self):
+            copy(self.src, self.dst, self.sem).wait()
+
+    third = [Halves(wg_hbm, wg, sem_k.at[0]), Halves(wu_hbm, wu, sem_k.at[1]), Halves(wd_hbm, wd, sem_k.at[2])]
 
     class Fetch:
         def __init__(self, hbm, buf, sem, c):
@@ -109,12 +115,18 @@
 
     def rs_copy(c, j):
         return pltpu.make_async_remote_copy(
-            src_ref=sbuf.at[c, peer(j)], dst_ref=rbuf.at[c, j - 1], send_sem=rs_s.at[c], recv_sem=rs_r.at[c],
+            src_ref=sbuf.at[c, peer(j)], dst_ref=rbuf.at[c, j - 1], send_sem=rs_s, recv_sem=rs_r.at[c],
             device_id={"tp": peer(j)})
+
+    ends = [sum(PASSES[:p + 1]) for p in range(len(PASSES))]
+    parts = [(hi - count, hi) for hi, count in zip(ends, PASSES)]
+
+    def pass_of(c):
+        return sum((c >= hi) * 1 for hi in ends[:-1])
 
     def ag_copy(c, j):
         return pltpu.make_async_remote_copy(
-            src_ref=hbuf.at[c, me], dst_ref=hbuf.at[c, me], send_sem=ag_s.at[c], recv_sem=ag_r.at[c],
+            src_ref=hbuf.at[c, me], dst_ref=hbuf.at[c, me], send_sem=ag_s, recv_sem=ag_r.at[pass_of(c)],
             device_id={"tp": peer(j)})
 
     def all_of(ref, sem):
@@ -216,7 +228,7 @@
 
         @pl.when(c + 1 == chunks)
         def _():
-            for cp in third[:4]:
+            for cp in third[:2]:
                 cp.start()
 
         with jax.named_scope("attend"):
@@ -241,8 +253,7 @@
     with jax.named_scope("v_wait"):
         for c in rest_of:
             fetch_v(c).wait()
-        for cp in third[4:]:
-            cp.start()
+        third[2].start()
     with jax.named_scope("mix"):
         o = [[mixed(c, g, wbuf[c % AHEAD, g]) for g in range(groups)] for c in rest_of]
         for c in rest_of:
@@ -252,13 +263,11 @@
             send(c)
     finish(chunks - 3)
 
-    ends = [sum(PASSES[:p + 1]) for p in range(len(PASSES))]
-    parts = [(hi - count, hi) for hi, count in zip(ends, PASSES)]
     gmv = gm[...].astype(F32)
 
     def rs2_copy(p, j):
         return pltpu.make_async_remote_copy(
-            src_ref=passes[4 * p + 1].at[peer(j)], dst_ref=passes[4 * p + 2].at[j - 1], send_sem=rs2_s.at[p],
+            src_ref=passes[4 * p + 1].at[peer(j)], dst_ref=passes[4 * p + 2].at[j - 1], send_sem=rs2_s,
             recv_sem=rs2_r.at[p], device_id={"tp": peer(j)})
 
     def own_part(p):
@@ -267,15 +276,14 @@
 
     def ag2_copy(p, j):
         return pltpu.make_async_remote_copy(
-            src_ref=passes[4 * p + 3], dst_ref=own_part(p), send_sem=ag2_s.at[p], recv_sem=ag2_r.at[p],
+            src_ref=passes[4 * p + 3], dst_ref=own_part(p), send_sem=ag2_s, recv_sem=ag2_r.at[p],
             device_id={"tp": peer(j)})
 
     def feed(p, lo, hi, between=None, after=()):
         p2, s2 = passes[4 * p:4 * p + 2]
         count = (hi - lo) * CH
         with jax.named_scope("ag_wait"):
-            for c in range(lo, hi):
-                all_of(rbuf.at[c], ag_r.at[c])
+            all_of(rbuf.at[pl.ds(lo, hi - lo)], ag_r.at[p])
 
         def h_block(j):
             return hbuf[lo:hi, j].astype(F32).reshape(count, blk)
@@ -295,7 +303,7 @@
                     bbuf[at_rows, 128 * g:128 * g + 128] = (hj[:, 128 * i:128 * i + 128] * scale * gmv[g:g + 1]).astype(BF16)
         if p == 0:
             with jax.named_scope("w_wait"):
-                for cp in third[:4]:
+                for cp in third[:2]:
                     cp.wait()
         with jax.named_scope("mlp"):
             hidden = []
@@ -309,8 +317,7 @@
             finish(between)
         if p == 0:
             with jax.named_scope("w_wait"):
-                for cp in third[4:]:
-                    cp.wait()
+                third[2].wait()
         with jax.named_scope("down"):
             for j in range(n):
                 part = dot(hidden, wd[:, blk * j:blk * (j + 1)])
@@ -344,15 +351,11 @@
     for p, (lo, hi) in enumerate(parts):
         finish2(p, lo, hi)
     with jax.named_scope("sends_wait"):
-        for c in range(chunks):
-            all_of(rbuf.at[c], rs_s.at[c])
-            all_of(rbuf.at[c], ag_s.at[c])
+        for sem in (rs_s, ag_s, rs2_s, ag2_s):
+            all_of(rbuf, sem)
     for p in range(len(PASSES)):
-        r2 = passes[4 * p + 2]
-        all_of(r2, rs2_s.at[p])
-        all_of(r2, ag2_s.at[p])
         with jax.named_scope("ag2_wait"):
-            all_of(r2, ag2_r.at[p])
+            all_of(passes[4 * p + 2], ag2_r.at[p])
 
 
 def put_out(y_ref, out_ref, sem):
@@ -412,9 +415,8 @@
                 pltpu.VMEM((chunks, n, CH, blk), BF16),
                 pltpu.VMEM((rows, d), BF16),
                 *second_half,
-                dma((12,)), dma((SLOTS,)), dma((SLOTS,)),
-                dma((chunks,)), dma((chunks,)), dma((chunks,)), dma((chunks,)),
-                *[dma((len(PASSES),))] * 4,
+                dma(()), dma((SLOTS,)), dma((SLOTS,)),
+                dma(()), dma((chunks,)), dma(()), *[dma((len(PASSES),)), dma(())] * 2, dma((len(PASSES),)),
             ],
             compiler_params=pltpu.CompilerParams(
                 collective_id=0, has_side_effects=True, vmem_limit_bytes=64336 * 1024),

time: 50.2 us -> 50 us (level)
  no operation moved by 1% of the time
where the time goes in v5:
time: 50 us; the launch traced here: 49.8 us
  Pallas kernels  49.8 us (100%)
    pallas_call x1, Pallas kernels, step(): pl.pallas_call(functools.partial(kernel, n), out_shape=pltpu.VMEM((rows,...  49.1 us

profile of v5, /device:TPU:22, one launch (start us, length us, event | category | flops | bytes accessed | tf_op | source)
XLA Modules:
  0.0 49.8 jit_solution(9942275988348164893)
XLA Ops:
  0.0 49.1 %decoder_layer.1.y_ref = bf16[64,2048]{1,0:T(8,128)(2,1)S(1)} custom-call(bf16[64,2048]{1,0:T(8,128)(2,1)} %x_hbm.1, bf16[64,2048,128]{2,1,0:T(8,128)(2,1)} %bitcast.4, bf16[64,2048,128]{2,1,0:T(8,128)(2,1)} %bitcast.5, bf16[16,128]{1,0:T(8,128)(2,1)} %bitcast.6, bf16[2048,256]{1,0:T(8,128)(2,1)} %wq_hbm.1, bf16[256,2048]{1,0:T(8,128)(2,1)} %wo_hbm.1, ...), custom_call_target="tpu_custom_call" | custom-call | tf_op jit(solution)/shard_map/decoder_layer/pallas_call | solution.py:392
  49.1 0.7 %put_out.1 = bf16[64,2048]{1,0:T(8,128)(2,1)} custom-call(bf16[64,2048]{1,0:T(8,128)(2,1)S(1)} %decoder_layer.1.y_ref), custom_call_target="tpu_custom_call" | custom-call | tf_op jit(solution)/shard_map/put_out/pallas_call | solution.py:425

commit v6 on v5

--- a/solution.py
+++ b/solution.py
@@ -14,7 +14,6 @@
 
 CH = 8
 SLOTS = 3
-AHEAD = 1
 LAG = 2
 GROUP = 4
 PASSES = (4, 2, 2)
@@ -184,16 +183,19 @@
             o = t if o is None else o + t
         return o[:tall // 2, :HEAD] + o[tall // 2:, HEAD:]
 
-    def project(c, o):
+    def project(*made):
         upper = lax.broadcasted_iota(jnp.int32, (CH, HEAD), 0) < GROUP
-        head0 = jnp.where(upper, o[0], pltpu.roll(o[1], GROUP, 0))
-        head1 = jnp.where(upper, pltpu.roll(o[0], GROUP, 0), o[1])
-        seen = jnp.concatenate([head0, head1], 1).astype(BF16)
-        term = dot(seen, wo[...])
-        for j in range(n):
-            part = term[:, blk * j:blk * (j + 1)]
-            pf[c, j] = part
-            sbuf[c, j] = part.astype(BF16)
+        seen = []
+        for _, o in made:
+            head0 = jnp.where(upper, o[0], pltpu.roll(o[1], GROUP, 0))
+            head1 = jnp.where(upper, pltpu.roll(o[0], GROUP, 0), o[1])
+            seen.append(jnp.concatenate([head0, head1], 1))
+        term = dot(jnp.concatenate(seen, 0).astype(BF16), wo[...])
+        for i, (c, _) in enumerate(made):
+            for j in range(n):
+                part = term[CH * i:CH * (i + 1), blk * j:blk * (j + 1)]
+                pf[c, j] = part
+                sbuf[c, j] = part.astype(BF16)
 
     def send(c):
         for j in far_first:
@@ -204,7 +206,7 @@
         fetch_k(2).start()
     with jax.named_scope("weigh"):
         for g in range(groups):
-            wbuf[0, g] = softmaxed(scored(0, g))
+            wbuf[g] = softmaxed(scored(0, g))
     with jax.named_scope("wait_wo"):
         for cp in second:
             cp.wait()
@@ -212,33 +214,25 @@
         pl.semaphore_wait(barrier, n - 1)
 
     def attend(c, _):
-        ready = c - AHEAD
+        ready = c - 1
         with jax.named_scope("k_wait"):
             fetch_k(c).wait()
         with jax.named_scope("v_wait"):
             fetch_v(ready).wait()
 
-        @pl.when(c + 1 < chunks)
-        def _():
-            fetch_v(c + 1).start()
+        fetch_v(c + 1).start()
 
         @pl.when(c + 2 < chunks)
         def _():
             fetch_k(c + 2).start()
 
-        @pl.when(c + 1 == chunks)
-        def _():
-            for cp in third[:2]:
-                cp.start()
-
         with jax.named_scope("attend"):
-            at = lax.rem(c, AHEAD)
-            before = [wbuf[at, g] for g in range(groups)]
+            before = [wbuf[g] for g in range(groups)]
             scores = [scored(c, g) for g in range(groups)]
             o = [mixed(ready, g, before[g]) for g in range(groups)]
             for g in range(groups):
-                wbuf[at, g] = softmaxed(scores[g])
-            project(ready, o)
+                wbuf[g] = softmaxed(scores[g])
+            project((ready, o))
         with jax.named_scope("send"):
             send(ready)
 
@@ -248,26 +242,36 @@
 
         return 0
 
-    lax.fori_loop(AHEAD, chunks, attend, 0)
-    rest_of = range(chunks - AHEAD, chunks)
+    lax.fori_loop(1, chunks - 1, attend, 0)
+
+    c = chunks - 1
+    with jax.named_scope("k_wait"):
+        fetch_k(c).wait()
+        fetch_v(c - 1).wait()
+        for cp in third[:2]:
+            cp.start()
+    with jax.named_scope("attend"):
+        before = [wbuf[g] for g in range(groups)]
+        scores = [scored(c, g) for g in range(groups)]
+        early = [mixed(c - 1, g, before[g]) for g in range(groups)]
+        for g in range(groups):
+            wbuf[g] = softmaxed(scores[g])
     with jax.named_scope("v_wait"):
-        for c in rest_of:
-            fetch_v(c).wait()
+        fetch_v(c).wait()
         third[2].start()
     with jax.named_scope("mix"):
-        o = [[mixed(c, g, wbuf[c % AHEAD, g]) for g in range(groups)] for c in rest_of]
-        for c in rest_of:
-            project(c, o[c - rest_of[0]])
+        project((c - 1, early), (c, [mixed(c, g, wbuf[g]) for g in range(groups)]))
     with jax.named_scope("send"):
-        for c in rest_of:
-            send(c)
-    finish(chunks - 3)
+        send(c - 1)
+        send(c)
+    finish(c - 1 - LAG)
+    finish(c - LAG)
 
     gmv = gm[...].astype(F32)
 
     def rs2_copy(p, j):
         return pltpu.make_async_remote_copy(
-            src_ref=passes[4 * p + 1].at[peer(j)], dst_ref=passes[4 * p + 2].at[j - 1], send_sem=rs2_s,
+            src_ref=passes[4 * p + 1].at[j - 1], dst_ref=passes[4 * p + 2].at[j - 1], send_sem=rs2_s,
             recv_sem=rs2_r.at[p], device_id={"tp": peer(j)})
 
     def own_part(p):
@@ -318,23 +322,32 @@
         if p == 0:
             with jax.named_scope("w_wait"):
                 third[2].wait()
-        with jax.named_scope("down"):
-            for j in range(n):
-                part = dot(hidden, wd[:, blk * j:blk * (j + 1)])
-                p2[j] = part
-                s2[j] = part.astype(BF16)
-        for c in after:
-            finish(c)
-        with jax.named_scope("send2"):
-            for j in far_first:
-                rs2_copy(p, j).start()
+        order = far_first + [0]
+        cut = 3 if p == len(PASSES) - 1 else n
+        for some in (order[:cut], order[cut:]):
+            with jax.named_scope("down"):
+                for j in some:
+                    part = dot(hidden, wd[:, pl.ds(pl.multiple_of(peer(j) * blk, blk), blk)])
+                    if j == 0:
+                        p2[...] = part
+                    else:
+                        s2[j - 1] = part.astype(BF16)
+            if cut == n:
+                for c in after:
+                    finish(c)
+            with jax.named_scope("send2"):
+                for j in some:
+                    if j > 0:
+                        rs2_copy(p, j).start()
+            if cut == n:
+                break
 
     def finish2(p, lo, hi):
         p2, _, r2, ybuf = passes[4 * p:4 * p + 4]
         with jax.named_scope("rs2_wait"):
             all_of(r2, rs2_r.at[p])
         with jax.named_scope("sum2"):
-            total = p2[me]
+            total = p2[...]
             for j in range(n - 1):
                 total = total + r2[j].astype(F32)
             total = total + hbuf[lo:hi, me].astype(F32).reshape((hi - lo) * CH, blk)
@@ -383,8 +396,8 @@
         assert sum(PASSES) == chunks
         for count in (CH * p for p in PASSES):
             second_half += [
-                pltpu.VMEM((n, count, blk), F32),
-                pltpu.VMEM((n, count, blk), BF16),
+                pltpu.VMEM((count, blk), F32),
+                pltpu.VMEM((n - 1, count, blk), BF16),
                 pltpu.VMEM((n - 1, count, blk), BF16),
                 pltpu.VMEM((count, blk), BF16),
             ]
@@ -408,7 +421,7 @@
                 pltpu.VMEM((SLOTS, CH, cache * heads, head), BF16),
                 pltpu.VMEM((SLOTS, CH, cache * heads, head), BF16),
                 pltpu.VMEM((rows // GROUP, heads * GROUP, head), F32),
-                pltpu.VMEM((AHEAD, CH // GROUP, 4 * GROUP, cache * heads // 2), F32),
+                pltpu.VMEM((CH // GROUP, 4 * GROUP, cache * heads // 2), F32),
                 pltpu.VMEM((chunks, n, CH, blk), F32),
                 pltpu.VMEM((chunks, n, CH, blk), BF16),
                 pltpu.VMEM((chunks, n - 1, CH, blk), BF16),

time: 50 us -> 49.7 us (level)
  no operation moved by 1% of the time
where the time goes in v6:
time: 49.7 us; the launch traced here: 49.6 us
  Pallas kernels  49.6 us (100%)
    pallas_call x1, Pallas kernels, step(): pl.pallas_call(functools.partial(kernel, n), out_shape=pltpu.VMEM((rows,...  48.9 us

profile of v6, /device:TPU:22, one launch (start us, length us, event | category | flops | bytes accessed | tf_op | source)
XLA Modules:
  0.0 49.6 jit_solution(3720054655362416112)
XLA Ops:
  0.0 48.9 %decoder_layer.1.y_ref = bf16[64,2048]{1,0:T(8,128)(2,1)S(1)} custom-call(bf16[64,2048]{1,0:T(8,128)(2,1)} %x_hbm.1, bf16[64,2048,128]{2,1,0:T(8,128)(2,1)} %bitcast.4, bf16[64,2048,128]{2,1,0:T(8,128)(2,1)} %bitcast.5, bf16[16,128]{1,0:T(8,128)(2,1)} %bitcast.6, bf16[2048,256]{1,0:T(8,128)(2,1)} %wq_hbm.1, bf16[256,2048]{1,0:T(8,128)(2,1)} %wo_hbm.1, ...), custom_call_target="tpu_custom_call" | custom-call | tf_op jit(solution)/shard_map/decoder_layer/pallas_call | solution.py:405
  48.9 0.7 %put_out.1 = bf16[64,2048]{1,0:T(8,128)(2,1)} custom-call(bf16[64,2048]{1,0:T(8,128)(2,1)S(1)} %decoder_layer.1.y_ref), custom_call_target="tpu_custom_call" | custom-call | tf_op jit(solution)/shard_map/put_out/pallas_call | solution.py:438

commit v7 on v6

--- a/solution.py
+++ b/solution.py
@@ -143,6 +143,29 @@
             for j in far_first:
                 ag_copy(c, j).start()
 
+    late = pl.ds(chunks - 2, 2)
+
+    def finish_late():
+        with jax.named_scope("finish_wait"):
+            all_of(rbuf.at[late], rs_r.at[chunks - 2])
+        with jax.named_scope("finish"):
+            for c in (chunks - 2, chunks - 1):
+                total = pf[c, me]
+                for j in range(n - 1):
+                    total = total + rbuf[c, j].astype(F32)
+                total = total + xf[c * CH:(c + 1) * CH, pl.ds(pl.multiple_of(me * blk, blk), blk)]
+                hbuf[c, me] = total.astype(BF16)
+            for j in far_first:
+                pltpu.make_async_remote_copy(
+                    src_ref=hbuf.at[late, me], dst_ref=hbuf.at[late, me], send_sem=ag_s,
+                    recv_sem=ag_r.at[len(PASSES) - 1], device_id={"tp": peer(j)}).start()
+
+    def send_late():
+        for j in far_first:
+            pltpu.make_async_remote_copy(
+                src_ref=sbuf.at[late, peer(j)], dst_ref=rbuf.at[late, j - 1], send_sem=rs_s,
+                recv_sem=rs_r.at[chunks - 2], device_id={"tp": peer(j)}).start()
+
     tall = 4 * GROUP
     row = lax.broadcasted_iota(jnp.int32, (tall, 2 * HEAD), 0)
     row_w = lax.broadcasted_iota(jnp.int32, (tall, span), 0)
@@ -262,8 +285,7 @@
     with jax.named_scope("mix"):
         project((c - 1, early), (c, [mixed(c, g, wbuf[g]) for g in range(groups)]))
     with jax.named_scope("send"):
-        send(c - 1)
-        send(c)
+        send_late()
     finish(c - 1 - LAG)
     finish(c - LAG)
 
@@ -283,7 +305,7 @@
             src_ref=passes[4 * p + 3], dst_ref=own_part(p), send_sem=ag2_s, recv_sem=ag2_r.at[p],
             device_id={"tp": peer(j)})
 
-    def feed(p, lo, hi, between=None, after=()):
+    def feed(p, lo, hi, between=None, after=None):
         p2, s2 = passes[4 * p:4 * p + 2]
         count = (hi - lo) * CH
         with jax.named_scope("ag_wait"):
@@ -332,9 +354,8 @@
                         p2[...] = part
                     else:
                         s2[j - 1] = part.astype(BF16)
-            if cut == n:
-                for c in after:
-                    finish(c)
+            if after is not None:
+                after()
             with jax.named_scope("send2"):
                 for j in some:
                     if j > 0:
@@ -358,7 +379,7 @@
 
     for p, (lo, hi) in enumerate(parts):
         if p == 0:
-            feed(p, lo, hi, None, (chunks - 2, chunks - 1))
+            feed(p, lo, hi, None, finish_late)
         else:
             feed(p, lo, hi)
     for p, (lo, hi) in enumerate(parts):
@@ -393,7 +414,7 @@
         keys = k_cache.reshape(batch, cache * heads, head)
         values = v_cache.reshape(batch, cache * heads, head)
         second_half = []
-        assert sum(PASSES) == chunks
+        assert sum(PASSES) == chunks and PASSES[-1] == 2
         for count in (CH * p for p in PASSES):
             second_half += [
                 pltpu.VMEM((count, blk), F32),
@@ -429,7 +450,7 @@
                 pltpu.VMEM((rows, d), BF16),
                 *second_half,
                 dma(()), dma((SLOTS,)), dma((SLOTS,)),
-                dma(()), dma((chunks,)), dma(()), *[dma((len(PASSES),)), dma(())] * 2, dma((len(PASSES),)),
+                dma(()), dma((chunks - 1,)), dma(()), *[dma((len(PASSES),)), dma(())] * 2, dma((len(PASSES),)),
             ],
             compiler_params=pltpu.CompilerParams(
                 collective_id=0, has_side_effects=True, vmem_limit_bytes=64336 * 1024),

time: 49.7 us -> 49.4 us (level)
  no operation moved by 1% of the time
where the time goes in v7:
time: 49.4 us; the launch traced here: 49.2 us
  Pallas kernels  49.2 us (100%)
    pallas_call x1, Pallas kernels, step(): pl.pallas_call(functools.partial(kernel, n), out_shape=pltpu.VMEM((rows,...  48.5 us

profile of v7, /device:TPU:22, one launch (start us, length us, event | category | flops | bytes accessed | tf_op | source)
XLA Modules:
  0.0 49.2 jit_solution(6475041225273649795)
XLA Ops:
  0.0 48.5 %decoder_layer.1.y_ref = bf16[64,2048]{1,0:T(8,128)(2,1)S(1)} custom-call(bf16[64,2048]{1,0:T(8,128)(2,1)} %x_hbm.1, bf16[64,2048,128]{2,1,0:T(8,128)(2,1)} %bitcast.4, bf16[64,2048,128]{2,1,0:T(8,128)(2,1)} %bitcast.5, bf16[16,128]{1,0:T(8,128)(2,1)} %bitcast.6, bf16[2048,256]{1,0:T(8,128)(2,1)} %wq_hbm.1, bf16[256,2048]{1,0:T(8,128)(2,1)} %wo_hbm.1, ...), custom_call_target="tpu_custom_call" | custom-call | tf_op jit(solution)/shard_map/decoder_layer/pallas_call | solution.py:426
  48.5 0.7 %put_out.1 = bf16[64,2048]{1,0:T(8,128)(2,1)} custom-call(bf16[64,2048]{1,0:T(8,128)(2,1)S(1)} %decoder_layer.1.y_ref), custom_call_target="tpu_custom_call" | custom-call | tf_op jit(solution)/shard_map/put_out/pallas_call | solution.py:459
